TPU v7x, 32 devices: a whole 2x2x4 slice. The times are simulated.
32 devices in a mesh: tok: 8 (over z, y), voc: 4 (over x, core).
Axes of the slice: x: 2, y: 2, z: 4, core: 2. Of those that a mesh axis runs over, the one named last changes fastest.
Arguments:
- hidden: bfloat16 [96, 4096], P(('tok', 'voc'))
- head_weight: bfloat16 [4096, 16032], P(None, ('tok', 'voc'))
- actions: int32 [96], P(('tok', 'voc')), may hold values from 0 to 16031
- old_logp: bfloat16 [96], P(('tok', 'voc')), may hold values from -80 to 1
- advantage: bfloat16 [96], P(('tok', 'voc')), may hold values from -4 to 4
- loss_mask: int32 [96], P(('tok', 'voc')), may hold values 0 or 1
Outputs:
- grad_weight: bfloat16 [4096, 16032], P(None, ('tok', 'voc'))
- grad_hidden: float32 [96, 4096], P(('tok', 'voc'))
All inputs are finite; a program needn't handle non-finite values. No bound on the sum of `loss_mask` on one device may be relied on, other than what follows from the above.
Results may differ from a plain program's by a relative error of at most 0.0047.
Values may be sent and summed in bfloat16 or wider, within the bound.
A program may use at most 128 MiB of HBM per device.

v0:
```python
import jax
import jax.numpy as jnp
from jax import lax
from jax.sharding import PartitionSpec as P


def per_device(hidden, head_weight, actions, old_logp, advantage, loss_mask):
    hidden_all, old_all, advant_all = (
        lax.all_gather(hidden, ("tok", "voc"), axis=0, tiled=True),
        lax.all_gather(old_logp, ("tok", "voc"), axis=0, tiled=True),
        lax.all_gather(advantage, ("tok", "voc"), axis=0, tiled=True),
    )
    action_all, mask_all = (
        lax.all_gather(actions, ("tok", "voc"), axis=0, tiled=True),
        lax.all_gather(loss_mask, ("tok", "voc"), axis=0, tiled=True),
    )
    width = head_weight.shape[1]
    logits = jnp.dot(hidden_all, head_weight, preferred_element_type=jnp.float32)
    first_col = lax.axis_index(("tok", "voc")) * width
    columns = first_col + lax.broadcasted_iota(jnp.int32, logits.shape, 1)
    matches = columns == action_all[:, None]
    target_part = jnp.sum(jnp.where(matches, logits, 0.0), axis=1)
    top = lax.pmax(jnp.max(logits, axis=1), ("tok", "voc"))
    shifted = jnp.exp(logits - top[:, None])
    sumexp, moment, target = lax.psum(
        (jnp.sum(shifted, axis=1), jnp.sum(shifted * logits, axis=1), target_part), ("tok", "voc")
    )
    lse = top + jnp.log(sumexp)
    mean_logit = moment / sumexp
    advant = advant_all.astype(jnp.float32)
    ratio = jnp.exp(target - lse - old_all.astype(jnp.float32))
    clipped = (advant > 0.0) & (ratio > 1.2) | (advant < 0.0) & (ratio < 0.8)
    active = jnp.where(clipped, 0.0, 1.0).astype(jnp.float32)
    weights = mask_all.astype(jnp.float32)
    policy = -advant * ratio * active * weights
    probability = jnp.exp(logits - lse[:, None])
    onehot = matches.astype(jnp.float32)
    dlogits = policy[:, None] * (onehot - probability) + 0.05 * weights[:, None] * probability * (
        logits - mean_logit[:, None]
    )
    dlogits = dlogits.astype(jnp.bfloat16)
    partial_rows = lax.psum_scatter(
        lax.dot_general(
            dlogits, head_weight, (((1,), (1,)), ((), ())), preferred_element_type=jnp.float32
        ),
        "tok",
        scatter_dimension=0,
        tiled=True,
    )
    grad_hidden = lax.psum_scatter(partial_rows, "voc", scatter_dimension=0, tiled=True)
    grad_weight = lax.dot_general(
        hidden_all, dlogits, (((0,), (0,)), ((), ())), preferred_element_type=jnp.float32
    ).astype(jnp.bfloat16)
    return (grad_weight, grad_hidden)


def solution(mesh):
    placed = (
        P(("tok", "voc"), None),
        P(None, ("tok", "voc")),
        P(("tok", "voc")),
        P(("tok", "voc")),
        P(("tok", "voc")),
        P(("tok", "voc")),
    )
    return jax.shard_map(
        per_device,
        mesh=mesh,
        in_specs=placed,
        out_specs=(P(None, ("tok", "voc")), P(("tok", "voc"), None)),
        check_vma=False,
    )
```

profile of v0, /device:TPU:0, one launch (start us, length us, event | category | flops | bytes accessed | tf_op | source)
XLA Modules:
  0.0 323.1 jit_solution(7266715647205631639)
XLA Ops:
  7.2 0.0 copy-start.1
  7.2 0.0 copy-start.2
  7.2 0.0 copy-start.3
  7.2 0.0 copy-start.4
  7.2 0.0 all-reduce.12.cloned.1.call-start
  7.3 46.5 %all-gather = bf16[32,3,4096]{2,1,0:T(4,128)(2,1)S(1)} all-gather(bf16[1,3,4096]{2,1,0:T(4,128)(2,1)} %bitcast.11), channel_id=1, replica_groups=mesh['tok'=8,'voc'=4] {'tok','voc'}, dimensions={0}, use_global_device_ids=true | all-gather | bytes 811008 | tf_op jit(solution)/shard_map/all_gather | solution.py:9
  53.7 0.7 reshape.20
  54.4 3.6 %fusion.12 = (f32[96]{0:T(128)S(1)}, f32[96,501]{1,0:T(8,128)S(1)}) fusion(bf16[96,4096]{1,0:T(8,128)(2,1)S(1)} %reshape.20, bf16[4096,501]{0,1:T(8,128)(2,1)} %param.7), kind=kOutput, calls=%fused_computation.21 | convolution fusion | flops 394050432 | bytes 5083392 | tf_op jit(solution)/shard_map/dot_general | solution.py:18
  58.0 36.9 %pmax.7 = f32[96]{0:T(128)S(1)} all-reduce(f32[96]{0:T(128)S(1)} %get-tuple-element.16), channel_id=1, replica_groups=mesh['tok'=8,'voc'=4] {'tok','voc'}, use_global_device_ids=true, to_apply=%region_3.4 | all-reduce | flops 96 | bytes 768 | tf_op jit(solution)/shard_map/pmax | solution.py:23
  94.9 0.0 copy-done.1
  94.9 0.2 dynamic-update-slice.2
  95.1 0.0 copy-done.2
  95.1 0.2 dynamic-update-slice
  95.4 41.1 %all-reduce.9 = (bf16[96]{0:T(256)(128)(2,1)S(1)}, bf16[96]{0:T(256)(128)(2,1)S(1)}) all-reduce(bf16[96]{0:T(256)(128)(2,1)S(1)} %dynamic-update-slice.2, bf16[96]{0:T(256)(128)(2,1)S(1)} %dynamic-update-slice), channel_id=1, replica_groups=mesh['tok'=8,'voc'=4] {'tok','voc'}, use_global_device_ids=true, to_apply=%add.2 | all-reduce | flops 192 | bytes 768
  136.5 0.0 copy-done.3
  136.5 0.2 dynamic-update-slice.1
  136.7 0.0 copy-done.4
  136.7 0.2 dynamic-update-slice.3
  137.0 39.5 %all-reduce.7 = (s32[96]{0:T(128)S(1)}, s32[96]{0:T(128)S(1)}) all-reduce(s32[96]{0:T(128)S(1)} %dynamic-update-slice.1, s32[96]{0:T(128)S(1)} %dynamic-update-slice.3), channel_id=1, replica_groups=mesh['tok'=8,'voc'=4] {'tok','voc'}, use_global_device_ids=true, to_apply=%add.1 | all-reduce | flops 192 | bytes 1536
  176.4 0.2 fusion.7
  176.7 40.5 %all-reduce.8 = (f32[96]{0:T(128)S(1)}, f32[96]{0:T(128)S(1)}, f32[96]{0:T(128)S(1)}) all-reduce(f32[96]{0:T(128)S(1)} %get-tuple-element.3, f32[96]{0:T(128)S(1)} %get-tuple-element.2, f32[96]{0:T(128)S(1)} %get-tuple-element.4), channel_id=1, replica_groups=mesh['tok'=8,'voc'=4] {'tok','voc'}, use_global_device_ids=true, to_apply=%region_7.8 | all-reduce | flops 288 | bytes 2304 | tf_op jit(solution)/shard_map/psum | solution.py:25
  217.1 0.0 copy-start
  217.2 3.2 fusion.9
  220.3 46.1 %fusion = f32[16,4096]{1,0:T(8,128)S(1)} fusion(f32[96,4096]{1,0:T(8,128)S(1)} %fusion.9), kind=kCustom, calls=%all-reduce-scatter | all-reduce-scatter fusion | flops 524289 | bytes 1835520
  266.5 4.3 %collective-permute-start = (f32[16,4096]{1,0:T(8,128)S(1)}, f32[16,4096]{1,0:T(8,128)S(1)}, u32[]{:S(2)}, u32[]{:S(2)}) collective-permute-start(f32[16,4096]{1,0:T(8,128)S(1)} %fusion), channel_id=1, source_target_pairs={{0,4},{4,8},{8,12},{12,16},{16,20},{20,24},{24,28},{1,5},{5,9},{9,... | collective-permute-start | bytes 786440
  270.8 2.7 collective-permute-start.1
  273.5 0.0 copy-done
  273.5 0.6 dynamic-slice.6
  274.7 2.6 collective-permute-done.1
  277.3 0.0 collective-permute-done
  277.3 0.6 concatenate
  278.0 0.0 copy-start.5
  278.0 0.7 constant_dynamic-slice_fusion
  278.7 0.0 all-reduce.12.cloned.1.call-update
  278.7 3.4 %fusion.1 = bf16[4096,501]{0,1:T(8,128)(2,1)} fusion(bf16[96,4096]{1,0:T(8,128)(2,1)S(1)} %reshape.20, f32[96,501]{1,0:T(8,128)S(1)} %get-tuple-element.17, f32[96]{0:T(128)S(1)} %get-tuple-element.14, f32[96]{0:T(128)S(1)} %get-tuple-element.15, f32[96]{0:T(128)S(1)} %get-tuple-element.13, f32[96]{0:T(128)S(1)} %get-tuple-element.12, ...), kind=kOutput, calls=%fused_computation.1 | convolution fusion | flops 396535488 | bytes 5086932 | tf_op jit(solution)/shard_map/dot_general | solution.py:51
  282.1 0.0 copy-done.5
  282.1 0.6 dynamic-slice.2
  283.4 31.4 %all-reduce.12.cloned.1.call-done = f32[12,4096]{1,0:T(8,128)} async-done(((f32[12,4096]{1,0:T(8,128)}), f32[12,4096]{1,0:T(8,128)}) %all-reduce.12.cloned.1.call-update) | async-done | bytes 196624
  314.7 1.6 constant_dynamic-slice_fusion.1
  (7 shorter events, 0.1 us)
Async XLA Ops:
  7.2 87.7 %copy-start.1 = (bf16[3]{0:T(256)(128)(2,1)S(1)}, bf16[3]{0:T(256)(128)(2,1)}, u32[]{:S(2)}) copy-start(bf16[3]{0:T(256)(128)(2,1)} %param.9) | copy-start | bytes 22
  7.2 88.0 %copy-start.2 = (bf16[3]{0:T(256)(128)(2,1)S(1)}, bf16[3]{0:T(256)(128)(2,1)}, u32[]{:S(2)}) copy-start(bf16[3]{0:T(256)(128)(2,1)} %param.10) | copy-start | bytes 22
  7.2 129.3 %copy-start.3 = (s32[3]{0:T(128)S(1)}, s32[3]{0:T(128)}, u32[]{:S(2)}) copy-start(s32[3]{0:T(128)} %param.8) | copy-start | bytes 40
  7.2 129.5 %copy-start.4 = (s32[3]{0:T(128)S(1)}, s32[3]{0:T(128)}, u32[]{:S(2)}) copy-start(s32[3]{0:T(128)} %param.11) | copy-start | bytes 40
  7.2 307.5 %all-reduce.12.cloned.1.call-start = ((), (), s32[]{:S(2)}) async-start(), calls=%async_computation | async-start | bytes 524288
  217.1 56.3 %copy-start = (u32[32]{0:T(128)S(1)}, u32[32]{0:T(128)}, u32[]{:S(2)}) copy-start(u32[32]{0:T(128)} %constant.50) | copy-start | bytes 388
  266.5 10.9 %collective-permute-start = (f32[16,4096]{1,0:T(8,128)S(1)}, f32[16,4096]{1,0:T(8,128)S(1)}, u32[]{:S(2)}, u32[]{:S(2)}) collective-permute-start(f32[16,4096]{1,0:T(8,128)S(1)} %fusion), channel_id=1, source_target_pairs={{0,4},{4,8},{8,12},{12,16},{16,20},{20,24},{24,28},{1,5},{5,9},{9,... | collective-permute-start | bytes 786440
  270.8 6.6 %collective-permute-start.1 = (f32[12,4096]{1,0:T(8,128)S(1)}, f32[12,4096]{1,0:T(8,128)S(1)}, u32[]{:S(2)}, u32[]{:S(2)}) collective-permute-start(f32[12,4096]{1,0:T(8,128)S(1)} %slice), channel_id=1, source_target_pairs={{0,8},{4,12},{8,16},{12,20},{16,24},{20,28},{1,9},{5,13},{9,17},{1... | collective-permute-start | bytes 589832
  278.0 4.1 %copy-start.5 = (u32[32]{0:T(128)S(1)}, u32[32]{0:T(128)}, u32[]{:S(2)}) copy-start(u32[32]{0:T(128)} %constant.54) | copy-start | bytes 388
Sparse Core Ops, SparseCore 0:
  278.9 35.7 all-reduce.11
where the time goes:
time: 324 us; the launch traced here: 323 us
  blocking collectives  251 us (77%)
  waiting for transfers between devices  34 us (10%)
  between operations  15.5 us (5%)
  matrix products  10.2 us (3%)
  starting transfers between devices  7 us (2%)
  local copies, waits for them, and re-layouts  5.77 us (2%)
    unnamed x3, blocking collectives  127 us
    all_gather x1, blocking collectives, per_device(): lax.all_gather(hidden, ('tok', 'voc'), axis=0, tiled=True)  46.5 us
    psum x1, blocking collectives, per_device(): lax.psum((jnp.sum(shifted, axis=1), jnp.sum(shifted * logits, axis=1), ta...  40.5 us
    pmax x1, blocking collectives, per_device(): top = lax.pmax(jnp.max(logits, axis=1), ('tok', 'voc'))  36.9 us
    unnamed x4, waiting for transfers between devices  34 us
    unnamed x3, starting transfers between devices  7 us
  transfers between devices with their start and end apart: 3, of which 2 were waited for; matrix products, arithmetic and copies ran while one was open for 1% of the time, Pallas kernels for 0%

commit v1 on v0

v1 whole, which is shorter than its diff:
```python
import functools

import jax
import jax.numpy as jnp
from jax import lax
from jax.experimental import pallas as pl
from jax.experimental.pallas import tpu as pltpu
from jax.sharding import PartitionSpec as P

MESH = pl.DeviceIdType.MESH
F32, BF16 = jnp.float32, jnp.bfloat16
LANES = 128


def step_of(size, most):
    best = LANES
    for k in range(LANES, most + 1, LANES):
        if size % k == 0:
            best = k
    return best


def kernel(dims, real, hx_ref, wt_hbm, gh_ref, dt_ref, gall_ref,
           wt, slab, stage, g, own, stats, logit, pb, rc, ra1, ra2, rb1, rb2, q, rz,
           w_sem, zs, zr, s1, r1, s2, r2, cs, cr, ss, sr, ks, kr, t1s, t1r, t2s, t2r, us, ur):
    Z, Y, X, C = dims
    n = Z * Y * X * C
    V = X * C
    rp = hx_ref.shape[0]
    width, D = wt.shape
    R = Z * rp
    T = n * rp
    tok, voc = lax.axis_index("tok"), lax.axis_index("voc")
    z, y = tok // Y, lax.rem(tok, Y)
    x, c = voc // C, lax.rem(voc, C)
    me = tok * V + voc

    load = pltpu.make_async_copy(wt_hbm, wt, w_sem)
    load.start()

    def device(zz, yy, xx, cc):
        return (zz * Y + yy, xx * C + cc)

    def at_offset(k):
        other = lax.rem(me + k, n)
        return (other // V, lax.rem(other, V))

    barrier = pltpu.get_barrier_semaphore()

    def greet(k, carry):
        pl.semaphore_signal(barrier, inc=1, device_id=at_offset(k), device_id_type=MESH)
        return carry

    lax.fori_loop(1, n, greet, 0)
    pl.semaphore_wait(barrier, n - 1)

    started = []

    def send(src, dst, ssem, rsem, dev):
        copy = pltpu.make_async_remote_copy(
            src_ref=src, dst_ref=dst, send_sem=ssem, recv_sem=rsem, device_id=dev, device_id_type=MESH
        )
        copy.start()
        started.append(copy)
        return copy

    line = [
        send(hx_ref, slab.at[z], zs.at[k], zr.at[k], device(lax.rem(z + k, Z), y, x, c))
        for k in range(1, Z)
    ]
    slab[z] = hx_ref[...]
    for copy in line:
        copy.wait_recv()
    for zi in range(Z):
        stage[zi * rp:(zi + 1) * rp, :] = slab[zi].astype(F32)
    g[c, x, y] = stage[...].astype(BF16)

    half = (D // 2) // LANES * LANES
    cuts = (pl.ds(0, half), pl.ds(half, g.shape[-1] - half))
    gcuts = (pl.ds(0, half), pl.ds(half, D - half))
    passed = []

    def share(slot, where):
        for k in range(1, C):
            i = len(passed)
            passed.append(send(g.at[(c,) + where], g.at[(c,) + where], cs.at[i], cr.at[i],
                               device(z, y, x, lax.rem(c + k, C))))

    def plane_device(part, k1, k2):
        if part == 0:
            return device(z, lax.rem(y + k1, Y), lax.rem(x + k2, X), c)
        return device(z, lax.rem(y + k2, Y), lax.rem(x + k1, X), c)

    sizes = ((Y, X), (X, Y))
    mine = ((y, x), (x, y))

    def block(part, a, b):
        return (b, a) if part == 0 else (a, b)

    first, second = [[], []], [[], []]
    for part in (0, 1):
        a, b = mine[part]
        where = block(part, a, b) + (slice(None), cuts[part])
        for k in range(1, sizes[part][0]):
            first[part].append(send(g.at[(c,) + where], g.at[(c,) + where], s1.at[part, k], r1.at[part, k],
                                    plane_device(part, k, 0)))
    for part in (0, 1):
        share(part, block(part, *mine[part]) + (slice(None), cuts[part]))
    for part in (0, 1):
        a, b = mine[part]
        for copy in first[part]:
            copy.wait_recv()
        where = block(part, slice(None), b) + (slice(None), cuts[part])
        for k in range(1, sizes[part][1]):
            second[part].append(send(g.at[(c,) + where], g.at[(c,) + where], s2.at[part, k], r2.at[part, k],
                                     plane_device(part, 0, k)))
    for part in (0, 1):
        a, b = mine[part]
        for k in range(1, sizes[part][0]):
            share(part, block(part, lax.rem(a + k, sizes[part][0]), b) + (slice(None), cuts[part]))
    for part in (0, 1):
        a, b = mine[part]
        for k in range(1, sizes[part][1]):
            second[part][k - 1].wait_recv()
            came = lax.rem(b + sizes[part][1] - k, sizes[part][1])
            share(part, block(part, slice(None), came) + (slice(None), cuts[part]))
    load.wait()
    for copy in passed:
        copy.wait_recv()

    kk = step_of(D, 512)
    logit[...] = jnp.zeros(logit.shape, F32)

    def add_depth(i, carry):
        cols = pl.ds(pl.multiple_of(i * kk, kk), kk)
        rows = g[:, :, :, :, cols].reshape(T, kk)
        logit[...] += lax.dot_general(wt[:, cols], rows, (((1,), (1,)), ((), ())), preferred_element_type=F32)
        return carry

    lax.fori_loop(0, D // kk, add_depth, 0)
    meta = g[:, :, :, :, D:D + LANES].reshape(T, LANES).astype(F32).T
    action = meta[0:1] + 256.0 * meta[1:2] + 65536.0 * meta[2:3]
    old, advant, weights = meta[3:4], meta[4:5], meta[5:6]

    logits = logit[...]
    column = (lax.broadcasted_iota(jnp.int32, (width, T), 0) + me * width).astype(F32)
    matches = column == action
    peak = jnp.max(logits, axis=0, keepdims=True)
    shifted = jnp.exp(logits - peak)
    own[0:1] = peak
    own[1:2] = jnp.sum(shifted, axis=0, keepdims=True)
    own[2:3] = jnp.sum(shifted * logits, axis=0, keepdims=True)
    own[3:4] = jnp.sum(jnp.where(matches, logits, 0.0), axis=0, keepdims=True)
    stats[0] = own[...]

    def stat_copy(k):
        return pltpu.make_async_remote_copy(
            src_ref=own, dst_ref=stats.at[k], send_sem=ss.at[k], recv_sem=sr.at[k],
            device_id=at_offset(k), device_id_type=MESH
        )

    def tell(k, carry):
        stat_copy(k).start()
        return carry

    def hear(k, carry):
        stat_copy(k).wait()
        return carry

    lax.fori_loop(1, n, tell, 0)
    lax.fori_loop(1, n, hear, 0)
    every = stats[...]
    top = jnp.max(every[:, 0:1, :], axis=0)
    total = jnp.sum(every * jnp.exp(every[:, 0:1, :] - top[None]), axis=0)
    target = jnp.sum(every[:, 3:4, :], axis=0)
    sumexp, moment = total[1:2], total[2:3]
    lse = top + jnp.log(sumexp)
    mean_logit = moment / sumexp
    ratio = jnp.exp(target - lse - old)
    clipped = ((advant > 0.0) & (ratio > 1.2)) | ((advant < 0.0) & (ratio < 0.8))
    active = jnp.where(clipped, 0.0, 1.0)
    policy = -advant * ratio * active * weights
    logits = logit[...]
    probability = jnp.exp(logits - lse)
    onehot = jnp.where(matches, 1.0, 0.0)
    dt = policy * (onehot - probability) + 0.05 * weights * probability * (logits - mean_logit)
    dt_ref[...] = dt.astype(BF16)
    d = dt.T.astype(BF16)

    halves = []
    for part in (0, 1):
        start, size = gcuts[part].start, gcuts[part].size
        cc = step_of(size, 512)

        def columns_of(i, carry):
            cols = pl.ds(pl.multiple_of(start + i * cc, LANES), cc)
            piece = jnp.dot(d, wt[:, cols], preferred_element_type=F32)
            pb[:, :, :, :, cols] = piece.astype(BF16).reshape(C, X, Y, R, cc)
            return carry

        lax.fori_loop(0, size // cc, columns_of, 0)
        halves.append([
            send(pb.at[lax.rem(c + k, C), :, :, :, gcuts[part]], rc.at[k, :, :, :, gcuts[part]],
                 ks.at[part, k], kr.at[part, k], device(z, y, x, lax.rem(c + k, C)))
            for k in range(1, C)
        ])

    lands1, lands2 = (ra1, rb1), (ra2, rb2)
    for part in (0, 1):
        cols = gcuts[part]
        for copy in halves[part]:
            copy.wait_recv()
        acc = pb[c, :, :, :, cols].astype(F32)
        for k in range(1, C):
            acc = acc + rc[k, :, :, :, cols].astype(F32)
        pb[c, :, :, :, cols] = acc.astype(BF16)
        a, b = mine[part]
        second[part] = []
        for k in range(1, sizes[part][1]):
            other = lax.rem(b + k, sizes[part][1])
            second[part].append(send(pb.at[(c,) + block(part, slice(None), other) + (slice(None), cols)],
                                     lands1[part].at[k], t1s.at[part, k], t1r.at[part, k], plane_device(part, 0, k)))
    for part in (0, 1):
        cols = gcuts[part]
        a, b = mine[part]
        here = (c,) + block(part, slice(None), b) + (slice(None), cols)
        for copy in second[part]:
            copy.wait_recv()
        acc = pb[here].astype(F32)
        for k in range(1, sizes[part][1]):
            acc = acc + lands1[part][k].astype(F32)
        pb[here] = acc.astype(BF16)
        first[part] = []
        for k in range(1, sizes[part][0]):
            other = lax.rem(a + k, sizes[part][0])
            first[part].append(send(pb.at[(c,) + block(part, other, b) + (slice(None), cols)],
                                    lands2[part].at[k], t2s.at[part, k], t2r.at[part, k], plane_device(part, k, 0)))
    for part in (0, 1):
        cols = gcuts[part]
        for copy in first[part]:
            copy.wait_recv()
        acc = pb[c, x, y, :, cols].astype(F32)
        for k in range(1, sizes[part][0]):
            acc = acc + lands2[part][k].astype(F32)
        stage[:, cols] = acc
    for zi in range(Z):
        q[zi] = stage[zi * rp:(zi + 1) * rp, 0:D].astype(BF16)
    line = [
        send(q.at[lax.rem(z + k, Z)], rz.at[k], us.at[k], ur.at[k], device(lax.rem(z + k, Z), y, x, c))
        for k in range(1, Z)
    ]
    gall_ref[...] = g[:, :, :, :, 0:D].reshape(T, D)
    acc = q[z].astype(F32)
    for k in range(1, Z):
        line[k - 1].wait_recv()
        acc = acc + rz[k].astype(F32)
    gh_ref[...] = acc[0:real]
    for copy in started:
        copy.wait_send()


def per_device(dims, hidden, head_weight, actions, old_logp, advantage, loss_mask):
    Z, Y, X, C = dims
    n = Z * Y * X * C
    real, D = hidden.shape
    width = head_weight.shape[1]
    rp = -(-real // 4) * 4
    while Z * rp % 16:
        rp += 4
    R, T = Z * rp, n * rp
    digits = (actions % 256, actions // 256 % 256, actions // 65536)
    vectors = [v.astype(BF16) for v in digits] + [old_logp, advantage, loss_mask.astype(BF16)]
    meta = jnp.pad(jnp.stack(vectors, axis=1), ((0, 0), (0, LANES - len(vectors))))
    hx = jnp.pad(jnp.concatenate([hidden, meta], axis=1), ((0, rp - real), (0, 0)))
    half = (D // 2) // LANES * LANES
    vmem = pl.BlockSpec(memory_space=pltpu.VMEM)
    dma = pltpu.SemaphoreType.DMA
    most = max(X, Y, Z, C)
    shared = (C - 1) * (2 + (Y - 1) + (X - 1) + (X - 1) + (Y - 1))
    grad_hidden, dt, gall = pl.pallas_call(
        functools.partial(kernel, dims, real),
        out_shape=(
            jax.ShapeDtypeStruct((real, D), F32),
            jax.ShapeDtypeStruct((width, T), BF16),
            jax.ShapeDtypeStruct((T, D), BF16),
        ),
        in_specs=[vmem, pl.BlockSpec(memory_space=pl.ANY)],
        out_specs=(vmem, vmem, vmem),
        scratch_shapes=[
            pltpu.VMEM((width, D), BF16),
            pltpu.VMEM((Z, rp, D + LANES), BF16),
            pltpu.VMEM((R, D + LANES), F32),
            pltpu.VMEM((C, X, Y, R, D + LANES), BF16),
            pltpu.VMEM((4, T), F32),
            pltpu.VMEM((n, 4, T), F32),
            pltpu.VMEM((width, T), F32),
            pltpu.VMEM((C, X, Y, R, D), BF16),
            pltpu.VMEM((C, X, Y, R, D), BF16),
            pltpu.VMEM((X, Y, R, half), BF16),
            pltpu.VMEM((Y, R, half), BF16),
            pltpu.VMEM((Y, X, R, D - half), BF16),
            pltpu.VMEM((X, R, D - half), BF16),
            pltpu.VMEM((Z, rp, D), BF16),
            pltpu.VMEM((Z, rp, D), BF16),
            dma,
            dma((Z,)), dma((Z,)),
            dma((2, most)), dma((2, most)),
            dma((2, most)), dma((2, most)),
            dma((max(shared, 1),)), dma((max(shared, 1),)),
            dma((n,)), dma((n,)),
            dma((2, most)), dma((2, most)),
            dma((2, most)), dma((2, most)),
            dma((2, most)), dma((2, most)),
            dma((Z,)), dma((Z,)),
        ],
        compiler_params=pltpu.CompilerParams(
            collective_id=0, has_side_effects=True, vmem_limit_bytes=60 * 1024 * 1024
        ),
    )(hx, head_weight.T)
    grad_weight = lax.dot_general(
        gall, dt, (((0,), (1,)), ((), ())), preferred_element_type=F32
    ).astype(BF16)
    return (grad_weight, grad_hidden)


def solution(mesh):
    tok, voc = mesh.shape["tok"], mesh.shape["voc"]
    inner = 2 if tok % 2 == 0 else 1
    cores = 2 if voc % 2 == 0 else 1
    dims = (tok // inner, inner, voc // cores, cores)
    placed = (
        P(("tok", "voc"), None),
        P(None, ("tok", "voc")),
        P(("tok", "voc")),
        P(("tok", "voc")),
        P(("tok", "voc")),
        P(("tok", "voc")),
    )
    return jax.shard_map(
        functools.partial(per_device, dims),
        mesh=mesh,
        in_specs=placed,
        out_specs=(P(None, ("tok", "voc")), P(("tok", "voc"), None)),
        check_vma=False,
    )
```

time: 324 us -> 56.9 us (0.18)
  blocking collectives: 251 us -> 0 us
  Pallas kernels: 0 us -> 46.1 us
  waiting for transfers between devices: 34 us -> 0 us
  between operations: 15.5 us -> 0.65 us
  starting transfers between devices: 7 us -> 0 us
  matrix products: 10.2 us -> 4.47 us
    unnamed x3 -> x0, blocking collectives: 127 us -> none
    all_gather x1 -> x0, blocking collectives: 46.5 us -> none  [per_device(): lax.all_gather(hidden, ('tok', 'voc'), axis=0, tiled=True)]
    pallas_call x0 -> x1, Pallas kernels: none -> 46.1 us  [per_device(): pl.pallas_call(functools.partial(kernel, dims, real), out_shape=(jax.Shap...]
    psum x1 -> x0, blocking collectives: 40.5 us -> none  [per_device(): lax.psum((jnp.sum(shifted, axis=1), jnp.sum(shifted * logits, axis=1), ta...]
    pmax x1 -> x0, blocking collectives: 36.9 us -> none  [per_device(): top = lax.pmax(jnp.max(logits, axis=1), ('tok', 'voc'))]
    unnamed x4 -> x0, waiting for transfers between devices: 34 us -> none
    unnamed x3 -> x0, starting transfers between devices: 7 us -> none
    dot_general x3 -> x1, matrix products: 10.2 us -> 4.47 us  [per_device(): lax.dot_general(gall, dt, (((0,), (1,)), ((), ())), preferred_element_typ...]
  transfers between devices with their start and end apart: 3 -> 0, of which waited for: 2 -> 0; matrix products, arithmetic and copies ran while one was open for 1% -> 0% of each run, Pallas kernels for 0% -> 0%
where the time goes in v1:
time: 56.9 us; the launch traced here: 56.6 us
  Pallas kernels  46.1 us (81%)
  matrix products  4.47 us (8%)
  local copies, waits for them, and re-layouts  3.31 us (6%)
  other arithmetic  2.11 us (4%)
  between operations  0.65 us (1%)
    pallas_call x1, Pallas kernels, per_device(): pl.pallas_call(functools.partial(kernel, dims, real), out_shape=(jax.Shap...  46.1 us
    dot_general x1, matrix products, per_device(): lax.dot_general(gall, dt, (((0,), (1,)), ((), ())), preferred_element_typ...  4.47 us
    another operation x7, local copies, waits for them, and re-layouts, per_device(): jnp.stack(vectors, axis=1)  2.04 us
    another operation x2, other arithmetic, per_device(): jnp.stack(vectors, axis=1)  1.33 us

profile of v1, /device:TPU:0, one launch (start us, length us, event | category | flops | bytes accessed | tf_op | source)
XLA Modules:
  0.0 56.6 jit_solution(4666990990888092906)
XLA Ops:
  0.6 0.7 %convert_bitcast_fusion = bf16[3,1]{0,1:T(2,128)(2,1)S(1)} fusion(s32[3]{0:T(128)} %param.11), kind=kLoop, calls=%fused_computation.20 | loop fusion | flops 3 | bytes 18 | tf_op jit(solution)/shard_map/stack | solution.py:273
  1.3 0.1 copy.13
  1.4 0.8 %copy.11 = bf16[3,1]{1,0:T(4,128)(2,1)S(1)} copy(bf16[3,1]{0,1:T(2,128)(2,1)} %bitcast.14) | data formatting | bytes 12 | tf_op jit(solution)/shard_map/stack | solution.py:273
  2.2 0.8 %copy.12 = bf16[3,1]{1,0:T(4,128)(2,1)S(1)} copy(bf16[3,1]{0,1:T(2,128)(2,1)} %bitcast.15) | data formatting | bytes 12 | tf_op jit(solution)/shard_map/stack | solution.py:273
  2.9 0.7 %convert_bitcast_fusion.1 = (bf16[3,1]{0,1:T(2,128)(2,1)S(1)}, bf16[3,1]{0,1:T(2,128)(2,1)S(1)}, bf16[3,1]{0,1:T(2,128)(2,1)S(1)}) fusion(s32[3]{0:T(128)} %param.8), kind=kLoop, calls=%fused_computation.21 | loop fusion | flops 129 | bytes 30 | tf_op jit(solution)/shard_map/stack | solution.py:273
  3.6 0.1 copy.10
  3.7 0.1 copy.8
  3.8 0.1 copy.9
  3.9 0.1 stack.27
  4.0 0.8 %fusion.1 = bf16[3,4224]{1,0:T(4,128)(2,1)S(1)} fusion(bf16[3,6]{1,0:T(4,128)(2,1)S(1)} %stack.27, bf16[3,4096]{1,0:T(4,128)(2,1)} %param.6), kind=kLoop, calls=%fused_computation.3 | loop fusion | flops 76032 | bytes 49956 | tf_op jit(solution)/shard_map/concatenate | solution.py:274
  4.8 0.6 %pad.9.hx_ref = bf16[4,4224]{1,0:T(4,128)(2,1)} pad(bf16[3,4224]{1,0:T(4,128)(2,1)S(1)} %fusion.1, bf16[]{:T(256)} %constant.46.clone.1), padding=0_1x0_0 | pad | bytes 59138 | tf_op jit(solution)/shard_map/jit(_pad)/pad | solution.py:274
  5.4 46.1 %shard_map.77 = (f32[3,4096]{1,0:T(4,128)}, bf16[501,128]{1,0:T(8,128)(2,1)}, bf16[128,4096]{1,0:T(8,128)(2,1)}) custom-call(bf16[4,4224]{1,0:T(4,128)(2,1)} %pad.9.hx_ref, bf16[501,4096]{1,0:T(8,128)(2,1)} %bitcast.13), custom_call_target="tpu_custom_call" | custom-call | tf_op jit(solution)/shard_map/pallas_call | solution.py:280
  51.5 0.0 copy-start
  51.5 4.5 %convolution_convert_fusion = bf16[4096,501]{0,1:T(8,128)(2,1)} fusion(bf16[128,4096]{1,0:T(8,128)(2,1)} %get-tuple-element.5, bf16[501,128]{1,0:T(8,128)(2,1)} %get-tuple-element.6), kind=kOutput, calls=%fused_computation | convolution fusion | flops 527388672 | bytes 5281024 | tf_op jit(solution)/shard_map/dot_general | solution.py:320
  56.0 0.0 copy-done
  56.0 0.6 %copy.15 = f32[3,4096]{1,0:T(4,128)} copy(f32[3,4096]{1,0:T(4,128)S(1)} %copy-done) | data formatting | bytes 98304
Async XLA Ops:
  51.5 4.5 %copy-start = (f32[3,4096]{1,0:T(4,128)S(1)}, f32[3,4096]{1,0:T(4,128)}, u32[]{:S(2)}) copy-start(f32[3,4096]{1,0:T(4,128)} %get-tuple-element.14) | copy-start | bytes 147460

commit v2 on v1

--- a/solution.py
+++ b/solution.py
@@ -1,4 +1,5 @@
 import functools
+import math
 
 import jax
 import jax.numpy as jnp
@@ -20,8 +21,8 @@
     return best
 
 
-def kernel(dims, real, hx_ref, wt_hbm, gh_ref, dt_ref, gall_ref,
-           wt, slab, stage, g, own, stats, logit, pb, rc, ra1, ra2, rb1, rb2, q, rz,
+def kernel(dims, real, hidden_ref, action_ref, mask_ref, pair_ref, wt_hbm, gh_ref, dt_ref, gall_ref,
+           wt, hx_ref, slab, stage, g, own, stats, logit, pb, rc, sb, ra1, ra2, rb1, rb2, q, qf, rz,
            w_sem, zs, zr, s1, r1, s2, r2, cs, cr, ss, sr, ks, kr, t1s, t1r, t2s, t2r, us, ur):
     Z, Y, X, C = dims
     n = Z * Y * X * C
@@ -52,6 +53,21 @@
         return carry
 
     lax.fori_loop(1, n, greet, 0)
+
+    lane = lax.broadcasted_iota(jnp.int32, (1, LANES), 1)
+    stage[0:rp, :] = jnp.zeros((rp, stage.shape[1]), F32)
+    stage[0:real, 0:D] = hidden_ref[...].astype(F32)
+    for r in range(real):
+        a = action_ref[r]
+        low, rest = lax.rem(a, 256), a // 256
+        whole = jnp.zeros((1, LANES), jnp.int32)
+        for at, value in enumerate((low, lax.rem(rest, 256), rest // 256)):
+            whole = jnp.where(lane == at, value, whole)
+        whole = jnp.where(lane == 5, mask_ref[r], whole)
+        extra = whole.astype(F32)
+        extra = jnp.where(lane == 3, pair_ref[r], extra)
+        stage[r:r + 1, D:D + LANES] = jnp.where(lane == 4, pair_ref[real + r], extra)
+    hx_ref[...] = stage[0:rp, :].astype(BF16)
     pl.semaphore_wait(barrier, n - 1)
 
     started = []
@@ -195,12 +211,12 @@
         def columns_of(i, carry):
             cols = pl.ds(pl.multiple_of(start + i * cc, LANES), cc)
             piece = jnp.dot(d, wt[:, cols], preferred_element_type=F32)
-            pb[:, :, :, :, cols] = piece.astype(BF16).reshape(C, X, Y, R, cc)
+            pb[:, :, :, :, cols] = piece.reshape(C, X, Y, R, cc)
             return carry
 
         lax.fori_loop(0, size // cc, columns_of, 0)
         halves.append([
-            send(pb.at[lax.rem(c + k, C), :, :, :, gcuts[part]], rc.at[k, :, :, :, gcuts[part]],
+            send(pb.at[lax.rem(c + k, C), :, :, :, gcuts[part]], rc.at[k - 1, :, :, :, gcuts[part]],
                  ks.at[part, k], kr.at[part, k], device(z, y, x, lax.rem(c + k, C)))
             for k in range(1, C)
         ])
@@ -210,47 +226,50 @@
         cols = gcuts[part]
         for copy in halves[part]:
             copy.wait_recv()
-        acc = pb[c, :, :, :, cols].astype(F32)
+        acc = pb[c, :, :, :, cols]
         for k in range(1, C):
-            acc = acc + rc[k, :, :, :, cols].astype(F32)
-        pb[c, :, :, :, cols] = acc.astype(BF16)
+            acc = acc + rc[k - 1, :, :, :, cols]
+        pb[c, :, :, :, cols] = acc
+        sb[:, :, :, cols] = acc.astype(BF16)
         a, b = mine[part]
         second[part] = []
         for k in range(1, sizes[part][1]):
             other = lax.rem(b + k, sizes[part][1])
-            second[part].append(send(pb.at[(c,) + block(part, slice(None), other) + (slice(None), cols)],
-                                     lands1[part].at[k], t1s.at[part, k], t1r.at[part, k], plane_device(part, 0, k)))
+            second[part].append(send(sb.at[block(part, slice(None), other) + (slice(None), cols)],
+                                     lands1[part].at[k - 1], t1s.at[part, k], t1r.at[part, k], plane_device(part, 0, k)))
     for part in (0, 1):
         cols = gcuts[part]
         a, b = mine[part]
-        here = (c,) + block(part, slice(None), b) + (slice(None), cols)
+        here = block(part, slice(None), b) + (slice(None), cols)
         for copy in second[part]:
             copy.wait_recv()
-        acc = pb[here].astype(F32)
+        acc = pb[(c,) + here]
         for k in range(1, sizes[part][1]):
-            acc = acc + lands1[part][k].astype(F32)
-        pb[here] = acc.astype(BF16)
+            acc = acc + lands1[part][k - 1].astype(F32)
+        pb[(c,) + here] = acc
+        sb[here] = acc.astype(BF16)
         first[part] = []
         for k in range(1, sizes[part][0]):
             other = lax.rem(a + k, sizes[part][0])
-            first[part].append(send(pb.at[(c,) + block(part, other, b) + (slice(None), cols)],
-                                    lands2[part].at[k], t2s.at[part, k], t2r.at[part, k], plane_device(part, k, 0)))
+            first[part].append(send(sb.at[block(part, other, b) + (slice(None), cols)],
+                                    lands2[part].at[k - 1], t2s.at[part, k], t2r.at[part, k], plane_device(part, k, 0)))
     for part in (0, 1):
         cols = gcuts[part]
         for copy in first[part]:
             copy.wait_recv()
-        acc = pb[c, x, y, :, cols].astype(F32)
+        acc = pb[c, x, y, :, cols]
         for k in range(1, sizes[part][0]):
-            acc = acc + lands2[part][k].astype(F32)
+            acc = acc + lands2[part][k - 1].astype(F32)
         stage[:, cols] = acc
     for zi in range(Z):
+        qf[zi] = stage[zi * rp:(zi + 1) * rp, 0:D]
         q[zi] = stage[zi * rp:(zi + 1) * rp, 0:D].astype(BF16)
     line = [
         send(q.at[lax.rem(z + k, Z)], rz.at[k], us.at[k], ur.at[k], device(lax.rem(z + k, Z), y, x, c))
         for k in range(1, Z)
     ]
     gall_ref[...] = g[:, :, :, :, 0:D].reshape(T, D)
-    acc = q[z].astype(F32)
+    acc = qf[z]
     for k in range(1, Z):
         line[k - 1].wait_recv()
         acc = acc + rz[k].astype(F32)
@@ -264,19 +283,39 @@
     n = Z * Y * X * C
     real, D = hidden.shape
     width = head_weight.shape[1]
-    rp = -(-real // 4) * 4
+    rp = real
     while Z * rp % 16:
-        rp += 4
+        rp += 1
     R, T = Z * rp, n * rp
-    digits = (actions % 256, actions // 256 % 256, actions // 65536)
-    vectors = [v.astype(BF16) for v in digits] + [old_logp, advantage, loss_mask.astype(BF16)]
-    meta = jnp.pad(jnp.stack(vectors, axis=1), ((0, 0), (0, LANES - len(vectors))))
-    hx = jnp.pad(jnp.concatenate([hidden, meta], axis=1), ((0, rp - real), (0, 0)))
+    pair = jnp.concatenate([old_logp, advantage]).astype(F32)
     half = (D // 2) // LANES * LANES
     vmem = pl.BlockSpec(memory_space=pltpu.VMEM)
+    smem = pl.BlockSpec(memory_space=pltpu.SMEM)
     dma = pltpu.SemaphoreType.DMA
     most = max(X, Y, Z, C)
     shared = (C - 1) * (2 + (Y - 1) + (X - 1) + (X - 1) + (Y - 1))
+    buffers = [
+        pltpu.VMEM((width, D), BF16),
+        pltpu.VMEM((rp, D + LANES), BF16),
+        pltpu.VMEM((Z, rp, D + LANES), BF16),
+        pltpu.VMEM((R, D + LANES), F32),
+        pltpu.VMEM((C, X, Y, R, D + LANES), BF16),
+        pltpu.VMEM((4, T), F32),
+        pltpu.VMEM((n, 4, T), F32),
+        pltpu.VMEM((width, T), F32),
+        pltpu.VMEM((C, X, Y, R, D), F32),
+        pltpu.VMEM((max(C - 1, 1), X, Y, R, D), F32),
+        pltpu.VMEM((X, Y, R, D), BF16),
+        pltpu.VMEM((max(X - 1, 1), Y, R, half), BF16),
+        pltpu.VMEM((max(Y - 1, 1), R, half), BF16),
+        pltpu.VMEM((max(Y - 1, 1), X, R, D - half), BF16),
+        pltpu.VMEM((max(X - 1, 1), R, D - half), BF16),
+        pltpu.VMEM((Z, rp, D), BF16),
+        pltpu.VMEM((Z, rp, D), F32),
+        pltpu.VMEM((Z, rp, D), BF16),
+    ]
+    taken = sum(math.prod(b.shape) * b.dtype.itemsize for b in buffers) + 2 * (width + D) * T
+    grant = min(taken * 5 // 4 + (8 << 20), 60 * 1024 * 1024)
     grad_hidden, dt, gall = pl.pallas_call(
         functools.partial(kernel, dims, real),
         out_shape=(
@@ -284,24 +323,10 @@
             jax.ShapeDtypeStruct((width, T), BF16),
             jax.ShapeDtypeStruct((T, D), BF16),
         ),
-        in_specs=[vmem, pl.BlockSpec(memory_space=pl.ANY)],
+        in_specs=[vmem, smem, smem, smem, pl.BlockSpec(memory_space=pltpu.HBM)],
         out_specs=(vmem, vmem, vmem),
         scratch_shapes=[
-            pltpu.VMEM((width, D), BF16),
-            pltpu.VMEM((Z, rp, D + LANES), BF16),
-            pltpu.VMEM((R, D + LANES), F32),
-            pltpu.VMEM((C, X, Y, R, D + LANES), BF16),
-            pltpu.VMEM((4, T), F32),
-            pltpu.VMEM((n, 4, T), F32),
-            pltpu.VMEM((width, T), F32),
-            pltpu.VMEM((C, X, Y, R, D), BF16),
-            pltpu.VMEM((C, X, Y, R, D), BF16),
-            pltpu.VMEM((X, Y, R, half), BF16),
-            pltpu.VMEM((Y, R, half), BF16),
-            pltpu.VMEM((Y, X, R, D - half), BF16),
-            pltpu.VMEM((X, R, D - half), BF16),
-            pltpu.VMEM((Z, rp, D), BF16),
-            pltpu.VMEM((Z, rp, D), BF16),
+            *buffers,
             dma,
             dma((Z,)), dma((Z,)),
             dma((2, most)), dma((2, most)),
@@ -314,9 +339,9 @@
             dma((Z,)), dma((Z,)),
         ],
         compiler_params=pltpu.CompilerParams(
-            collective_id=0, has_side_effects=True, vmem_limit_bytes=60 * 1024 * 1024
+            collective_id=0, has_side_effects=True, vmem_limit_bytes=grant
         ),
-    )(hx, head_weight.T)
+    )(hidden, actions, loss_mask, pair, head_weight.T)
     grad_weight = lax.dot_general(
         gall, dt, (((0,), (1,)), ((), ())), preferred_element_type=F32
     ).astype(BF16)

time: 56.9 us -> 55.4 us (0.974)
  local copies, waits for them, and re-layouts: 3.31 us -> 4.86 us
  other arithmetic: 2.11 us -> 0.75 us
  matrix products: 4.47 us -> 3.21 us
    unnamed x3 -> x9, local copies, waits for them, and re-layouts: 0.63 us -> 4.86 us
    another operation x7 -> x0, local copies, waits for them, and re-layouts: 2.04 us -> none  [per_device(): jnp.stack(vectors, axis=1)]
    another operation x2 -> x0, other arithmetic: 1.33 us -> none  [per_device(): jnp.stack(vectors, axis=1)]
    dot_general x1, matrix products: 4.47 us -> 3.21 us  [per_device(): lax.dot_general(gall, dt, (((0,), (1,)), ((), ())), preferred_element_typ...]
    concatenate x1 -> x0, other arithmetic: 0.78 us -> none  [per_device(): jnp.concatenate([hidden, meta], axis=1)]
    convert_element_type x0 -> x1, other arithmetic: none -> 0.75 us  [per_device(): pair = jnp.concatenate([old_logp, advantage]).astype(F32)]
    pad x1 -> x0, local copies, waits for them, and re-layouts: 0.63 us -> none  [per_device(): jnp.pad(jnp.concatenate([hidden, meta], axis=1), ((0, rp - real), (0, 0)))]
where the time goes in v2:
time: 55.4 us; the launch traced here: 55.2 us
  Pallas kernels  45.7 us (82%)
  local copies, waits for them, and re-layouts  4.86 us (9%)
  matrix products  3.21 us (6%)
  other arithmetic  0.75 us (1%)
  between operations  0.64 us (1%)
    pallas_call x1, Pallas kernels, per_device(): pl.pallas_call(functools.partial(kernel, dims, real), out_shape=(jax.Shap...  45.7 us
    unnamed x9, local copies, waits for them, and re-layouts  4.86 us
    dot_general x1, matrix products, per_device(): lax.dot_general(gall, dt, (((0,), (1,)), ((), ())), preferred_element_typ...  3.21 us

profile of v2, /device:TPU:0, one launch (start us, length us, event | category | flops | bytes accessed | tf_op | source)
XLA Modules:
  0.0 55.2 jit_solution(8655026162565593777)
XLA Ops:
  0.6 0.7 %maximum_convert_fusion.pair_ref = f32[6]{0:T(128)S(1)} fusion(bf16[3]{0:T(256)(128)(2,1)} %param.10, bf16[3]{0:T(256)(128)(2,1)} %param.9), kind=kLoop, calls=%fused_computation.1 | loop fusion | flops 24 | bytes 36 | tf_op jit(solution)/shard_map/convert_element_type | solution.py:290
  1.4 0.0 copy-start
  1.4 2.2 %copy-done = bf16[4096,501]{0,1:T(8,128)(2,1)S(1)} copy-done((bf16[4096,501]{0,1:T(8,128)(2,1)S(1)}, bf16[4096,501]{0,1:T(8,128)(2,1)}, u32[]{:S(2)}) %copy-start) | copy-done | bytes 4104216
  3.5 0.0 copy-start.1
  3.5 0.8 %copy-done.1 = bf16[3,4096]{1,0:T(4,128)(2,1)S(1)} copy-done((bf16[3,4096]{1,0:T(4,128)(2,1)S(1)}, bf16[3,4096]{1,0:T(4,128)(2,1)}, u32[]{:S(2)}) %copy-start.1) | copy-done | bytes 24600
  4.3 0.0 copy-start.2
  4.3 0.7 %copy-done.2 = s32[3]{0:T(128)S(1)} copy-done((s32[3]{0:T(128)S(1)}, s32[3]{0:T(128)}, u32[]{:S(2)}) %copy-start.2) | copy-done | bytes 36
  5.0 0.0 copy-start.3
  5.0 0.7 %copy-done.3 = s32[3]{0:T(128)S(1)} copy-done((s32[3]{0:T(128)S(1)}, s32[3]{0:T(128)}, u32[]{:S(2)}) %copy-start.3) | copy-done | bytes 36
  5.6 45.7 %shard_map.77 = (f32[3,4096]{1,0:T(4,128)S(1)}, bf16[501,128]{1,0:T(8,128)(2,1)S(1)}, bf16[128,4096]{1,0:T(8,128)(2,1)S(1)}) custom-call(bf16[3,4096]{1,0:T(4,128)(2,1)S(1)} %copy-done.1, s32[3]{0:T(128)S(1)} %copy-done.2, s32[3]{0:T(128)S(1)} %copy-done.3, f32[6]{0:T(128)S(1)} %maximum_convert_fusion.pair_ref, bf16[501,4096]{1,0:T(8,128)(2,1)S(1)} %bitcast.3), custom_call_target="tpu_custom_call" | custom-call | tf_op jit(solution)/shard_map/pallas_call | solution.py:319
  51.3 3.2 %convolution_convert_fusion = bf16[4096,501]{0,1:T(8,128)(2,1)} fusion(bf16[128,4096]{1,0:T(8,128)(2,1)S(1)} %get-tuple-element.5, bf16[501,128]{1,0:T(8,128)(2,1)S(1)} %get-tuple-element.6), kind=kOutput, calls=%fused_computation | convolution fusion | flops 527388672 | bytes 5281024 | tf_op jit(solution)/shard_map/dot_general | solution.py:345
  54.5 0.6 %copy.9 = f32[3,4096]{1,0:T(4,128)} copy(f32[3,4096]{1,0:T(4,128)S(1)} %get-tuple-element.11) | data formatting | bytes 98304
Async XLA Ops:
  1.4 2.2 %copy-start = (bf16[4096,501]{0,1:T(8,128)(2,1)S(1)}, bf16[4096,501]{0,1:T(8,128)(2,1)}, u32[]{:S(2)}) copy-start(bf16[4096,501]{0,1:T(8,128)(2,1)} %param.7) | copy-start | bytes 12312580
  3.5 0.8 %copy-start.1 = (bf16[3,4096]{1,0:T(4,128)(2,1)S(1)}, bf16[3,4096]{1,0:T(4,128)(2,1)}, u32[]{:S(2)}) copy-start(bf16[3,4096]{1,0:T(4,128)(2,1)} %hidden_ref.1) | copy-start | bytes 73732
  4.3 0.7 %copy-start.2 = (s32[3]{0:T(128)S(1)}, s32[3]{0:T(128)}, u32[]{:S(2)}) copy-start(s32[3]{0:T(128)} %action_ref.1) | copy-start | bytes 40
  5.0 0.7 %copy-start.3 = (s32[3]{0:T(128)S(1)}, s32[3]{0:T(128)}, u32[]{:S(2)}) copy-start(s32[3]{0:T(128)} %mask_ref.1) | copy-start | bytes 40

commit v3 on v2

v3 whole, which is shorter than its diff:
```python
import functools
import math

import jax
import jax.numpy as jnp
from jax import lax
from jax.experimental import pallas as pl
from jax.experimental.pallas import tpu as pltpu
from jax.sharding import PartitionSpec as P

MESH = pl.DeviceIdType.MESH
F32, BF16 = jnp.float32, jnp.bfloat16
LANES = 128
PARTS = 4


def step_of(size, most):
    best = LANES
    for k in range(LANES, most + 1, LANES):
        if size % k == 0:
            best = k
    return best


def waves(parts, stages, lag):
    pairs = [(p, s) for p in range(parts) for s in range(stages)]
    return sorted(pairs, key=lambda ps: (ps[0] + lag * ps[1], -ps[1]))


def part_columns(D, parts):
    size = D // parts // LANES * LANES
    edges = [p * size for p in range(parts)] + [D]
    return list(zip(edges[:-1], edges[1:]))


def kernel(dims, real, parts, hidden_hbm, action_hbm, mask_hbm, old_hbm, advant_hbm, wt_hbm, gh_ref, dt_ref, gall_ref,
           hidden_ref, action_ref, mask_ref, old_ref, advant_ref,
           wt, hx_ref, slab, stage, g, own, stats, logit, pb, rc, sb, q, qf, rz,
           in_sem, w_sem, zs, zr, s1, r1, s2, r2, cs, cr, ss, sr, ks, kr, t1s, t1r, t2s, t2r, us, ur, *lands):
    Z, Y, X, C = dims
    n = Z * Y * X * C
    V = X * C
    rp = hx_ref.shape[0]
    width, D = wt.shape
    R = Z * rp
    T = n * rp
    tok, voc = lax.axis_index("tok"), lax.axis_index("voc")
    z, y = tok // Y, lax.rem(tok, Y)
    x, c = voc // C, lax.rem(voc, C)
    me = tok * V + voc

    inputs = [
        pltpu.make_async_copy(src, dst, in_sem.at[i])
        for i, (src, dst) in enumerate((
            (hidden_hbm, hidden_ref), (action_hbm, action_ref), (mask_hbm, mask_ref),
            (old_hbm, old_ref), (advant_hbm, advant_ref),
        ))
    ]
    for copy in inputs:
        copy.start()
    load = pltpu.make_async_copy(wt_hbm, wt, w_sem)
    load.start()

    def device(zz, yy, xx, cc):
        return (zz * Y + yy, xx * C + cc)

    def at_offset(k):
        other = lax.rem(me + k, n)
        return (other // V, lax.rem(other, V))

    barrier = pltpu.get_barrier_semaphore()

    def greet(k, carry):
        pl.semaphore_signal(barrier, inc=1, device_id=at_offset(k), device_id_type=MESH)
        return carry

    lax.fori_loop(1, n, greet, 0)

    for copy in inputs:
        copy.wait()
    lane = lax.broadcasted_iota(jnp.int32, (1, LANES), 1)
    stage[0:rp, :] = jnp.zeros((rp, stage.shape[1]), F32)
    stage[0:real, 0:D] = hidden_ref[...].astype(F32)
    spot = lax.broadcasted_iota(jnp.int32, (1, real), 1)
    olds = old_ref[...].reshape(1, real).astype(F32)
    advants = advant_ref[...].reshape(1, real).astype(F32)
    for r in range(real):
        a = action_ref[r]
        low, rest = lax.rem(a, 256), a // 256
        whole = jnp.zeros((1, LANES), jnp.int32)
        for at, value in enumerate((low, lax.rem(rest, 256), rest // 256)):
            whole = jnp.where(lane == at, value, whole)
        whole = jnp.where(lane == 5, mask_ref[r], whole)
        extra = whole.astype(F32)
        for at, values in ((3, olds), (4, advants)):
            value = jnp.sum(jnp.where(spot == r, values, 0.0), axis=1, keepdims=True)
            extra = jnp.where(lane == at, value, extra)
        stage[r:r + 1, D:D + LANES] = extra
    hx_ref[...] = stage[0:rp, :].astype(BF16)
    pl.semaphore_wait(barrier, n - 1)

    started = []

    def send(src, dst, ssem, rsem, dev):
        copy = pltpu.make_async_remote_copy(
            src_ref=src, dst_ref=dst, send_sem=ssem, recv_sem=rsem, device_id=dev, device_id_type=MESH
        )
        copy.start()
        started.append(copy)
        return copy

    spans = part_columns(D, parts)
    gcuts = [pl.ds(a, b - a) for a, b in spans]
    cuts = gcuts[:-1] + [pl.ds(spans[-1][0], D + LANES - spans[-1][0])]
    sizes = [(Y, X) if p % 2 == 0 else (X, Y) for p in range(parts)]
    mine = [(y, x) if p % 2 == 0 else (x, y) for p in range(parts)]

    def block(p, a, b):
        return (b, a) if p % 2 == 0 else (a, b)

    def plane_device(p, k1, k2):
        dx, dy = block(p, k1, k2)
        return device(z, lax.rem(y + dy, Y), lax.rem(x + dx, X), c)

    passed = [[] for _ in range(parts)]

    def share(p, where):
        for k in range(1, C):
            i = len(passed[p])
            passed[p].append(send(g.at[(c,) + where], g.at[(c,) + where], cs.at[p, i], cr.at[p, i],
                                  device(z, y, x, lax.rem(c + k, C))))

    line = [
        [send(hx_ref.at[:, cuts[p]], slab.at[z, :, cuts[p]], zs.at[p, k], zr.at[p, k],
              device(lax.rem(z + k, Z), y, x, c)) for k in range(1, Z)]
        for p in range(parts)
    ]
    slab[z] = hx_ref[...]
    first, second = [[] for _ in range(parts)], [[] for _ in range(parts)]

    def multiply(p):
        begin, end = spans[p]
        kk = step_of(end - begin, 512)
        for at in range(begin, end, kk):
            cols = pl.ds(at, kk)
            rows = g[:, :, :, :, cols].reshape(T, kk)
            term = lax.dot_general(wt[:, cols], rows, (((1,), (1,)), ((), ())), preferred_element_type=F32)
            logit[...] = term if at == 0 else logit[...] + term

    for p, s in waves(parts, 4, 3):
        a, b = mine[p]
        if s == 0:
            for copy in line[p]:
                copy.wait_recv()
            for zi in range(Z):
                stage[zi * rp:(zi + 1) * rp, cuts[p]] = slab[zi, :, cuts[p]].astype(F32)
            g[c, x, y, :, cuts[p]] = stage[:, cuts[p]].astype(BF16)
            where = block(p, a, b) + (slice(None), cuts[p])
            for k in range(1, sizes[p][0]):
                first[p].append(send(g.at[(c,) + where], g.at[(c,) + where], s1.at[p, k], r1.at[p, k],
                                     plane_device(p, k, 0)))
            share(p, where)
        elif s == 1:
            for copy in first[p]:
                copy.wait_recv()
            where = block(p, slice(None), b) + (slice(None), cuts[p])
            for k in range(1, sizes[p][1]):
                second[p].append(send(g.at[(c,) + where], g.at[(c,) + where], s2.at[p, k], r2.at[p, k],
                                      plane_device(p, 0, k)))
            for k in range(1, sizes[p][0]):
                share(p, block(p, lax.rem(a + k, sizes[p][0]), b) + (slice(None), cuts[p]))
        elif s == 2:
            for k in range(1, sizes[p][1]):
                second[p][k - 1].wait_recv()
                came = lax.rem(b + sizes[p][1] - k, sizes[p][1])
                share(p, block(p, slice(None), came) + (slice(None), cuts[p]))
        else:
            if p == 0:
                load.wait()
            for copy in passed[p]:
                copy.wait_recv()
            multiply(p)

    meta = g[:, :, :, :, D:D + LANES].reshape(T, LANES).astype(F32).T
    action = meta[0:1] + 256.0 * meta[1:2] + 65536.0 * meta[2:3]
    old, advant, weights = meta[3:4], meta[4:5], meta[5:6]

    logits = logit[...]
    column = (lax.broadcasted_iota(jnp.int32, (width, T), 0) + me * width).astype(F32)
    matches = column == action
    peak = jnp.max(logits, axis=0, keepdims=True)
    shifted = jnp.exp(logits - peak)
    own[0:1] = peak
    own[1:2] = jnp.sum(shifted, axis=0, keepdims=True)
    own[2:3] = jnp.sum(shifted * logits, axis=0, keepdims=True)
    own[3:4] = jnp.sum(jnp.where(matches, logits, 0.0), axis=0, keepdims=True)
    stats[0] = own[...]

    def stat_copy(k):
        return pltpu.make_async_remote_copy(
            src_ref=own, dst_ref=stats.at[k], send_sem=ss.at[k], recv_sem=sr.at[k],
            device_id=at_offset(k), device_id_type=MESH
        )

    def tell(k, carry):
        stat_copy(k).start()
        return carry

    def hear(k, carry):
        stat_copy(k).wait()
        return carry

    lax.fori_loop(1, n, tell, 0)
    lax.fori_loop(1, n, hear, 0)
    every = stats[...]
    top = jnp.max(every[:, 0:1, :], axis=0)
    total = jnp.sum(every * jnp.exp(every[:, 0:1, :] - top[None]), axis=0)
    target = jnp.sum(every[:, 3:4, :], axis=0)
    sumexp, moment = total[1:2], total[2:3]
    lse = top + jnp.log(sumexp)
    mean_logit = moment / sumexp
    ratio = jnp.exp(target - lse - old)
    clipped = ((advant > 0.0) & (ratio > 1.2)) | ((advant < 0.0) & (ratio < 0.8))
    active = jnp.where(clipped, 0.0, 1.0)
    policy = -advant * ratio * active * weights
    logits = logit[...]
    probability = jnp.exp(logits - lse)
    onehot = jnp.where(matches, 1.0, 0.0)
    dt = policy * (onehot - probability) + 0.05 * weights * probability * (logits - mean_logit)
    dt_ref[...] = dt.astype(BF16)
    d = dt.T.astype(BF16)

    halves, line = [[] for _ in range(parts)], [[] for _ in range(parts)]
    first, second = [[] for _ in range(parts)], [[] for _ in range(parts)]
    for p, s in waves(parts, 5, 3):
        a, b = mine[p]
        cols = gcuts[p]
        here = block(p, slice(None), b) + (slice(None), cols)
        if s == 0:
            begin, end = spans[p]
            cc = step_of(end - begin, 512)
            for at in range(begin, end, cc):
                piece = jnp.dot(d, wt[:, at:at + cc], preferred_element_type=F32)
                pb[:, :, :, :, at:at + cc] = piece.reshape(C, X, Y, R, cc)
            halves[p] = [
                send(pb.at[lax.rem(c + k, C), :, :, :, cols], rc.at[k - 1, :, :, :, cols],
                     ks.at[p, k], kr.at[p, k], device(z, y, x, lax.rem(c + k, C)))
                for k in range(1, C)
            ]
        elif s == 1:
            for copy in halves[p]:
                copy.wait_recv()
            acc = pb[c, :, :, :, cols]
            for k in range(1, C):
                acc = acc + rc[k - 1, :, :, :, cols]
            pb[c, :, :, :, cols] = acc
            sb[:, :, :, cols] = acc.astype(BF16)
            for k in range(1, sizes[p][1]):
                other = lax.rem(b + k, sizes[p][1])
                second[p].append(send(sb.at[block(p, slice(None), other) + (slice(None), cols)],
                                      lands[2 * p].at[k - 1], t1s.at[p, k], t1r.at[p, k], plane_device(p, 0, k)))
        elif s == 2:
            for copy in second[p]:
                copy.wait_recv()
            acc = pb[(c,) + here]
            for k in range(1, sizes[p][1]):
                acc = acc + lands[2 * p][k - 1].astype(F32)
            pb[(c,) + here] = acc
            sb[here] = acc.astype(BF16)
            for k in range(1, sizes[p][0]):
                other = lax.rem(a + k, sizes[p][0])
                first[p].append(send(sb.at[block(p, other, b) + (slice(None), cols)],
                                     lands[2 * p + 1].at[k - 1], t2s.at[p, k], t2r.at[p, k], plane_device(p, k, 0)))
            if p == 0:
                gall_ref[...] = g[:, :, :, :, 0:D].reshape(T, D)
        elif s == 3:
            for copy in first[p]:
                copy.wait_recv()
            acc = pb[c, x, y, :, cols]
            for k in range(1, sizes[p][0]):
                acc = acc + lands[2 * p + 1][k - 1].astype(F32)
            stage[:, cols] = acc
            for zi in range(Z):
                piece = stage[zi * rp:(zi + 1) * rp, cols]
                qf[zi, :, cols] = piece
                q[zi, :, cols] = piece.astype(BF16)
            line[p] = [
                send(q.at[lax.rem(z + k, Z), :, cols], rz.at[k, :, cols], us.at[p, k], ur.at[p, k],
                     device(lax.rem(z + k, Z), y, x, c))
                for k in range(1, Z)
            ]
        else:
            acc = qf[z, :, cols]
            for k in range(1, Z):
                line[p][k - 1].wait_recv()
                acc = acc + rz[k, :, cols].astype(F32)
            gh_ref[:, cols] = acc[0:real]
    for copy in started:
        copy.wait_send()


def per_device(dims, hidden, head_weight, actions, old_logp, advantage, loss_mask):
    Z, Y, X, C = dims
    n = Z * Y * X * C
    real, D = hidden.shape
    width = head_weight.shape[1]
    rp = real
    while Z * rp % 16:
        rp += 1
    R, T = Z * rp, n * rp
    parts = PARTS
    spans = part_columns(D, parts)
    vmem = pl.BlockSpec(memory_space=pltpu.VMEM)
    hbm = pl.BlockSpec(memory_space=pltpu.HBM)
    dma = pltpu.SemaphoreType.DMA
    most = max(X, Y, Z, C)
    shared = max((C - 1) * (X + Y - 1), 1)
    lands = []
    for p, (begin, end) in enumerate(spans):
        one, two = (Y, X) if p % 2 == 0 else (X, Y)
        lands.append(pltpu.VMEM((max(two - 1, 1), one, R, end - begin), BF16))
        lands.append(pltpu.VMEM((max(one - 1, 1), R, end - begin), BF16))
    buffers = [
        pltpu.VMEM((width, D), BF16),
        pltpu.VMEM((rp, D + LANES), BF16),
        pltpu.VMEM((Z, rp, D + LANES), BF16),
        pltpu.VMEM((R, D + LANES), F32),
        pltpu.VMEM((C, X, Y, R, D + LANES), BF16),
        pltpu.VMEM((4, T), F32),
        pltpu.VMEM((n, 4, T), F32),
        pltpu.VMEM((width, T), F32),
        pltpu.VMEM((C, X, Y, R, D), F32),
        pltpu.VMEM((max(C - 1, 1), X, Y, R, D), F32),
        pltpu.VMEM((X, Y, R, D), BF16),
        pltpu.VMEM((Z, rp, D), BF16),
        pltpu.VMEM((Z, rp, D), F32),
        pltpu.VMEM((Z, rp, D), BF16),
    ]
    taken = sum(math.prod(b.shape) * b.dtype.itemsize for b in buffers + lands) + 2 * (width + D) * T
    grant = min(taken * 5 // 4 + (8 << 20), 60 * 1024 * 1024)
    grad_hidden, dt, gall = pl.pallas_call(
        functools.partial(kernel, dims, real, parts),
        out_shape=(
            jax.ShapeDtypeStruct((real, D), F32),
            jax.ShapeDtypeStruct((width, T), BF16),
            jax.ShapeDtypeStruct((T, D), BF16),
        ),
        in_specs=[hbm] * 6,
        out_specs=(vmem, vmem, vmem),
        scratch_shapes=[
            pltpu.VMEM(hidden.shape, BF16),
            pltpu.SMEM(actions.shape, jnp.int32),
            pltpu.SMEM(loss_mask.shape, jnp.int32),
            pltpu.VMEM(old_logp.shape, BF16),
            pltpu.VMEM(advantage.shape, BF16),
            *buffers,
            dma((5,)),
            dma,
            dma((parts, Z)), dma((parts, Z)),
            dma((parts, most)), dma((parts, most)),
            dma((parts, most)), dma((parts, most)),
            dma((parts, shared)), dma((parts, shared)),
            dma((n,)), dma((n,)),
            dma((parts, most)), dma((parts, most)),
            dma((parts, most)), dma((parts, most)),
            dma((parts, most)), dma((parts, most)),
            dma((parts, Z)), dma((parts, Z)),
            *lands,
        ],
        compiler_params=pltpu.CompilerParams(
            collective_id=0, has_side_effects=True, vmem_limit_bytes=grant
        ),
    )(*(pltpu.with_memory_space_constraint(v, pltpu.HBM)
        for v in (hidden, actions, loss_mask, old_logp, advantage, head_weight.T)))
    grad_weight = lax.dot_general(
        gall, dt, (((0,), (1,)), ((), ())), preferred_element_type=F32
    ).astype(BF16)
    return (grad_weight, grad_hidden)


def solution(mesh):
    tok, voc = mesh.shape["tok"], mesh.shape["voc"]
    inner = 2 if tok % 2 == 0 else 1
    cores = 2 if voc % 2 == 0 else 1
    dims = (tok // inner, inner, voc // cores, cores)
    placed = (
        P(("tok", "voc"), None),
        P(None, ("tok", "voc")),
        P(("tok", "voc")),
        P(("tok", "voc")),
        P(("tok", "voc")),
        P(("tok", "voc")),
    )
    return jax.shard_map(
        functools.partial(per_device, dims),
        mesh=mesh,
        in_specs=placed,
        out_specs=(P(None, ("tok", "voc")), P(("tok", "voc"), None)),
        check_vma=False,
    )
```

time: 55.4 us -> 51.2 us (0.924)
  local copies, waits for them, and re-layouts: 4.86 us -> 0.63 us
  Pallas kernels: 45.7 us -> 46.6 us
  other arithmetic: 0.75 us -> 0 us
    unnamed x9 -> x1, local copies, waits for them, and re-layouts: 4.86 us -> 0.63 us
    pallas_call x1, Pallas kernels: 45.7 us -> 46.6 us  [per_device(): pl.pallas_call(functools.partial(kernel, dims, real, parts), out_shape=(j...]
    convert_element_type x1 -> x0, other arithmetic: 0.75 us -> none  [per_device(): pair = jnp.concatenate([old_logp, advantage]).astype(F32)]
where the time goes in v3:
time: 51.2 us; the launch traced here: 51.1 us
  Pallas kernels  46.6 us (91%)
  matrix products  3.21 us (6%)
  between operations  0.64 us (1%)
  local copies, waits for them, and re-layouts  0.63 us (1%)
    pallas_call x1, Pallas kernels, per_device(): pl.pallas_call(functools.partial(kernel, dims, real, parts), out_shape=(j...  46.6 us
    dot_general x1, matrix products, per_device(): lax.dot_general(gall, dt, (((0,), (1,)), ((), ())), preferred_element_typ...  3.21 us

profile of v3, /device:TPU:0, one launch (start us, length us, event | category | flops | bytes accessed | tf_op | source)
XLA Modules:
  0.0 51.1 jit_solution(16903570201670028725)
XLA Ops:
  0.6 46.6 %shard_map.77 = (f32[3,4096]{1,0:T(4,128)S(1)}, bf16[501,128]{1,0:T(8,128)(2,1)S(1)}, bf16[128,4096]{1,0:T(8,128)(2,1)S(1)}) custom-call(bf16[3,4096]{1,0:T(4,128)(2,1)} %hidden_hbm.1, s32[3]{0:T(128)} %action_hbm.1, s32[3]{0:T(128)} %mask_hbm.1, bf16[3]{0:T(256)(128)(2,1)} %old_hbm.1, bf16[3]{0:T(256)(128)(2,1)} %advant_hbm.1, bf16[501,4096]{1,0:T(8,128)(2,1)} %bitcast.3), custom_call_target="tpu_custom_call" | custom-call | tf_op jit(solution)/shard_map/pallas_call | solution.py:341
  47.2 3.2 %convolution_convert_fusion = bf16[4096,501]{0,1:T(8,128)(2,1)} fusion(bf16[128,4096]{1,0:T(8,128)(2,1)S(1)} %get-tuple-element.5, bf16[501,128]{1,0:T(8,128)(2,1)S(1)} %get-tuple-element.6), kind=kOutput, calls=%fused_computation | convolution fusion | flops 527388672 | bytes 5281024 | tf_op jit(solution)/shard_map/dot_general | solution.py:375
  50.4 0.6 %copy.9 = f32[3,4096]{1,0:T(4,128)} copy(f32[3,4096]{1,0:T(4,128)S(1)} %get-tuple-element.11) | data formatting | bytes 98304

commit v4 on v3

--- a/solution.py
+++ b/solution.py
@@ -11,7 +11,9 @@
 MESH = pl.DeviceIdType.MESH
 F32, BF16 = jnp.float32, jnp.bfloat16
 LANES = 128
-PARTS = 4
+PARTS = 2
+GATHER_DELAYS = (0, 3, 6, 7.5)
+SCATTER_DELAYS = (0, 3, 6, 9, 12)
 
 
 def step_of(size, most):
@@ -22,9 +24,9 @@
     return best
 
 
-def waves(parts, stages, lag):
-    pairs = [(p, s) for p in range(parts) for s in range(stages)]
-    return sorted(pairs, key=lambda ps: (ps[0] + lag * ps[1], -ps[1]))
+def waves(parts, delays):
+    pairs = [(p, s) for p in range(parts) for s in range(len(delays))]
+    return sorted(pairs, key=lambda ps: (ps[0] + delays[ps[1]], -ps[1]))
 
 
 def part_columns(D, parts):
@@ -147,7 +149,7 @@
             term = lax.dot_general(wt[:, cols], rows, (((1,), (1,)), ((), ())), preferred_element_type=F32)
             logit[...] = term if at == 0 else logit[...] + term
 
-    for p, s in waves(parts, 4, 3):
+    for p, s in waves(parts, GATHER_DELAYS):
         a, b = mine[p]
         if s == 0:
             for copy in line[p]:
@@ -202,8 +204,8 @@
             device_id=at_offset(k), device_id_type=MESH
         )
 
-    def tell(k, carry):
-        stat_copy(k).start()
+    def tell(i, carry):
+        stat_copy(1 + lax.rem(i + n // 4, n - 1)).start()
         return carry
 
     def hear(k, carry):
@@ -232,7 +234,7 @@
 
     halves, line = [[] for _ in range(parts)], [[] for _ in range(parts)]
     first, second = [[] for _ in range(parts)], [[] for _ in range(parts)]
-    for p, s in waves(parts, 5, 3):
+    for p, s in waves(parts, SCATTER_DELAYS):
         a, b = mine[p]
         cols = gcuts[p]
         here = block(p, slice(None), b) + (slice(None), cols)

time: 51.2 us -> 47.8 us (0.934)
  Pallas kernels: 46.6 us -> 43.2 us
    pallas_call x1, Pallas kernels: 46.6 us -> 43.2 us  [per_device(): pl.pallas_call(functools.partial(kernel, dims, real, parts), out_shape=(j...]
where the time goes in v4:
time: 47.8 us; the launch traced here: 47.6 us
  Pallas kernels  43.2 us (90%)
  matrix products  3.21 us (7%)
  between operations  0.64 us (1%)
  local copies, waits for them, and re-layouts  0.63 us (1%)
    pallas_call x1, Pallas kernels, per_device(): pl.pallas_call(functools.partial(kernel, dims, real, parts), out_shape=(j...  43.2 us
    dot_general x1, matrix products, per_device(): lax.dot_general(gall, dt, (((0,), (1,)), ((), ())), preferred_element_typ...  3.21 us

profile of v4, /device:TPU:0, one launch (start us, length us, event | category | flops | bytes accessed | tf_op | source)
XLA Modules:
  0.0 47.6 jit_solution(16302702638025513217)
XLA Ops:
  0.6 43.2 %shard_map.77 = (f32[3,4096]{1,0:T(4,128)S(1)}, bf16[501,128]{1,0:T(8,128)(2,1)S(1)}, bf16[128,4096]{1,0:T(8,128)(2,1)S(1)}) custom-call(bf16[3,4096]{1,0:T(4,128)(2,1)} %hidden_hbm.1, s32[3]{0:T(128)} %action_hbm.1, s32[3]{0:T(128)} %mask_hbm.1, bf16[3]{0:T(256)(128)(2,1)} %old_hbm.1, bf16[3]{0:T(256)(128)(2,1)} %advant_hbm.1, bf16[501,4096]{1,0:T(8,128)(2,1)} %bitcast.3), custom_call_target="tpu_custom_call" | custom-call | tf_op jit(solution)/shard_map/pallas_call | solution.py:343
  43.8 3.2 %convolution_convert_fusion = bf16[4096,501]{0,1:T(8,128)(2,1)} fusion(bf16[128,4096]{1,0:T(8,128)(2,1)S(1)} %get-tuple-element.5, bf16[501,128]{1,0:T(8,128)(2,1)S(1)} %get-tuple-element.6), kind=kOutput, calls=%fused_computation | convolution fusion | flops 527388672 | bytes 5281024 | tf_op jit(solution)/shard_map/dot_general | solution.py:377
  47.0 0.6 %copy.9 = f32[3,4096]{1,0:T(4,128)} copy(f32[3,4096]{1,0:T(4,128)S(1)} %get-tuple-element.11) | data formatting | bytes 98304

commit v5 on v4

--- a/solution.py
+++ b/solution.py
@@ -35,9 +35,9 @@
     return list(zip(edges[:-1], edges[1:]))
 
 
-def kernel(dims, real, parts, hidden_hbm, action_hbm, mask_hbm, old_hbm, advant_hbm, wt_hbm, gh_ref, dt_ref, gall_ref,
+def kernel(dims, real, parts, hidden_hbm, action_hbm, mask_hbm, old_hbm, advant_hbm, wt_hbm, gh_ref, gw_ref,
            hidden_ref, action_ref, mask_ref, old_ref, advant_ref,
-           wt, hx_ref, slab, stage, g, own, stats, logit, pb, rc, sb, q, qf, rz,
+           wt, dt_ref, hx_ref, slab, stage, g, own, stats, logit, pb, rc, sb, q, qf, rz,
            in_sem, w_sem, zs, zr, s1, r1, s2, r2, cs, cr, ss, sr, ks, kr, t1s, t1r, t2s, t2r, us, ur, *lands):
     Z, Y, X, C = dims
     n = Z * Y * X * C
@@ -133,9 +133,7 @@
                                   device(z, y, x, lax.rem(c + k, C))))
 
     line = [
-        [send(hx_ref.at[:, cuts[p]], slab.at[z, :, cuts[p]], zs.at[p, k], zr.at[p, k],
-              device(lax.rem(z + k, Z), y, x, c)) for k in range(1, Z)]
-        for p in range(parts)
+        send(hx_ref, slab.at[z], zs.at[0, k], zr.at[0, k], device(lax.rem(z + k, Z), y, x, c)) for k in range(1, Z)
     ]
     slab[z] = hx_ref[...]
     first, second = [[] for _ in range(parts)], [[] for _ in range(parts)]
@@ -152,7 +150,7 @@
     for p, s in waves(parts, GATHER_DELAYS):
         a, b = mine[p]
         if s == 0:
-            for copy in line[p]:
+            for copy in line if p == 0 else ():
                 copy.wait_recv()
             for zi in range(Z):
                 stage[zi * rp:(zi + 1) * rp, cuts[p]] = slab[zi, :, cuts[p]].astype(F32)
@@ -232,6 +230,13 @@
     dt_ref[...] = dt.astype(BF16)
     d = dt.T.astype(BF16)
 
+    def weigh(p):
+        begin, end = spans[p]
+        cc = step_of(end - begin, 512)
+        for at in range(begin, end, cc):
+            rows = g[:, :, :, :, at:at + cc].reshape(T, cc)
+            gw_ref[:, at:at + cc] = jnp.dot(dt_ref[...], rows, preferred_element_type=F32).astype(BF16)
+
     halves, line = [[] for _ in range(parts)], [[] for _ in range(parts)]
     first, second = [[] for _ in range(parts)], [[] for _ in range(parts)]
     for p, s in waves(parts, SCATTER_DELAYS):
@@ -273,8 +278,6 @@
                 other = lax.rem(a + k, sizes[p][0])
                 first[p].append(send(sb.at[block(p, other, b) + (slice(None), cols)],
                                      lands[2 * p + 1].at[k - 1], t2s.at[p, k], t2r.at[p, k], plane_device(p, k, 0)))
-            if p == 0:
-                gall_ref[...] = g[:, :, :, :, 0:D].reshape(T, D)
         elif s == 3:
             for copy in first[p]:
                 copy.wait_recv()
@@ -297,6 +300,12 @@
                 line[p][k - 1].wait_recv()
                 acc = acc + rz[k, :, cols].astype(F32)
             gh_ref[:, cols] = acc[0:real]
+        if (p, s) == (parts - 1, 1):
+            for other in range(parts // 2):
+                weigh(other)
+        if (p, s) == (parts - 1, 2):
+            for other in range(parts // 2, parts):
+                weigh(other)
     for copy in started:
         copy.wait_send()
 
@@ -324,6 +333,7 @@
         lands.append(pltpu.VMEM((max(one - 1, 1), R, end - begin), BF16))
     buffers = [
         pltpu.VMEM((width, D), BF16),
+        pltpu.VMEM((width, T), BF16),
         pltpu.VMEM((rp, D + LANES), BF16),
         pltpu.VMEM((Z, rp, D + LANES), BF16),
         pltpu.VMEM((R, D + LANES), F32),
@@ -338,17 +348,16 @@
         pltpu.VMEM((Z, rp, D), F32),
         pltpu.VMEM((Z, rp, D), BF16),
     ]
-    taken = sum(math.prod(b.shape) * b.dtype.itemsize for b in buffers + lands) + 2 * (width + D) * T
+    taken = sum(math.prod(b.shape) * b.dtype.itemsize for b in buffers + lands) + 2 * width * D
     grant = min(taken * 5 // 4 + (8 << 20), 60 * 1024 * 1024)
-    grad_hidden, dt, gall = pl.pallas_call(
+    grad_hidden, grad_weight = pl.pallas_call(
         functools.partial(kernel, dims, real, parts),
         out_shape=(
             jax.ShapeDtypeStruct((real, D), F32),
-            jax.ShapeDtypeStruct((width, T), BF16),
-            jax.ShapeDtypeStruct((T, D), BF16),
+            jax.ShapeDtypeStruct((width, D), BF16),
         ),
         in_specs=[hbm] * 6,
-        out_specs=(vmem, vmem, vmem),
+        out_specs=(vmem, vmem),
         scratch_shapes=[
             pltpu.VMEM(hidden.shape, BF16),
             pltpu.SMEM(actions.shape, jnp.int32),
@@ -374,10 +383,7 @@
         ),
     )(*(pltpu.with_memory_space_constraint(v, pltpu.HBM)
         for v in (hidden, actions, loss_mask, old_logp, advantage, head_weight.T)))
-    grad_weight = lax.dot_general(
-        gall, dt, (((0,), (1,)), ((), ())), preferred_element_type=F32
-    ).astype(BF16)
-    return (grad_weight, grad_hidden)
+    return (grad_weight.T, grad_hidden)
 
 
 def solution(mesh):

time: 47.8 us -> 46.6 us (0.975)
  matrix products: 3.21 us -> 0 us
  local copies, waits for them, and re-layouts: 0.63 us -> 2.62 us
    dot_general x1 -> x0, matrix products: 3.21 us -> none  [per_device(): lax.dot_general(gall, dt, (((0,), (1,)), ((), ())), preferred_element_typ...]
    unnamed x1 -> x2, local copies, waits for them, and re-layouts: 0.63 us -> 2.62 us
where the time goes in v5:
time: 46.6 us; the launch traced here: 46.5 us
  Pallas kernels  43.2 us (93%)
  local copies, waits for them, and re-layouts  2.62 us (6%)
  between operations  0.64 us (1%)
    pallas_call x1, Pallas kernels, per_device(): pl.pallas_call(functools.partial(kernel, dims, real, parts), out_shape=(j...  43.2 us
    unnamed x2, local copies, waits for them, and re-layouts  2.62 us

profile of v5, /device:TPU:0, one launch (start us, length us, event | category | flops | bytes accessed | tf_op | source)
XLA Modules:
  0.0 46.5 jit_solution(9691696871261994268)
XLA Ops:
  0.6 43.2 %shard_map.77 = (f32[3,4096]{1,0:T(4,128)S(1)}, bf16[501,4096]{1,0:T(8,128)(2,1)S(1)}) custom-call(bf16[3,4096]{1,0:T(4,128)(2,1)} %hidden_hbm.1, s32[3]{0:T(128)} %action_hbm.1, s32[3]{0:T(128)} %mask_hbm.1, bf16[3]{0:T(256)(128)(2,1)} %old_hbm.1, bf16[3]{0:T(256)(128)(2,1)} %advant_hbm.1, bf16[501,4096]{1,0:T(8,128)(2,1)} %bitcast.3), custom_call_target="tpu_custom_call" | custom-call | tf_op jit(solution)/shard_map/pallas_call | solution.py:353
  43.8 2.0 %copy.10 = bf16[4096,501]{0,1:T(8,128)(2,1)} copy(bf16[4096,501]{0,1:T(8,128)(2,1)S(1)} %bitcast.2) | data formatting | bytes 8208384
  45.8 0.6 %copy.11 = f32[3,4096]{1,0:T(4,128)} copy(f32[3,4096]{1,0:T(4,128)S(1)} %get-tuple-element.9) | data formatting | bytes 98304
